TPU v7x, 512 devices: a whole 4x4x16 slice. The times are simulated.
512 devices in a mesh: leaf: 16 (over z_lo, core), grp: 8 (over y, z_hi), mrg: 4 (over x).
Axes of the slice: x: 4, y: 4, z: 16 (z_hi: 2, z_lo: 8; z = z_hi * 8 + z_lo), core: 2. Of those that a mesh axis runs over, the one named last changes fastest.
Arguments:
- row_owner: int32 [768], replicated, may hold values from 0 to 767, as said below
- face_left: float32 [8, 4, 768, 768], P('grp', 'mrg', 'leaf'), as said below
- face_cross: float32 [8, 4, 768, 768], P('grp', 'mrg', 'leaf')
- face_right: float32 [8, 4, 768, 768], P('grp', 'mrg', 'leaf')
Outputs:
- out_left: float32 [8, 4, 768, 768], P('grp', 'mrg', 'leaf')
- out_cross: float32 [8, 4, 768, 768], P('grp', 'mrg', 'leaf')
- out_right: float32 [8, 4, 768, 768], P('grp', 'mrg', 'leaf')
Inputs may be any that keep to these rules, and one draw needn't show every extreme that they name: row_owner holds each of the 768 face DOFs exactly once. `face_left`: for every box, the symmetric matrix [[L, C], [C^T, R]] built from natural rows is positive definite, L and R are symmetric.
All inputs are finite; a program needn't handle non-finite values.
Results may differ from a plain program's by a relative error of at most 0.0003.
Values sent between devices are 32-bit elements; how exact they have to be, the bound alone decides.
No kernel may reach another device: no remote copies, remote signals or barrier semaphores. Data moves between devices by JAX's collectives and lax.ppermute only.
A program may use at most 128 MiB of HBM per device.

v0:
```python
import jax
import jax.numpy as jnp
from jax import lax
from jax.sharding import PartitionSpec as P


def partner_2(block, axis, distance):
    count = lax.axis_size(axis)
    route = []
    for low in range(count):
        high = low | 1 << distance
        if high != low and high < count:
            route += [(low, high), (high, low)]
    return lax.ppermute(block, axis, route)


def dot_high(left, right):
    return jnp.dot(left, right, precision=lax.Precision.HIGHEST, preferred_element_type=jnp.float32)


def dot_against(left, right):
    return lax.dot_general(
        left,
        right,
        (((1,), (1,)), ((), ())),
        precision=lax.Precision.HIGHEST,
        preferred_element_type=jnp.float32,
    )


def dot_leading(left, right):
    return lax.dot_general(
        left,
        right,
        (((0,), (0,)), ((), ())),
        precision=lax.Precision.HIGHEST,
        preferred_element_type=jnp.float32,
    )


def arrange(mine, partner, role):
    first = jnp.where(role == 0, mine, partner)
    second = jnp.where(role == 0, partner, mine)
    return (first, second)


def merge_rows(first, second, factor, cross_left, cross_right, start):
    rows = first.shape[1]
    columns = lax.dynamic_slice_in_dim(cross_right, start, rows, 1)
    solved = jax.scipy.linalg.cho_solve((factor, True), first[1].T).T
    weights = jax.scipy.linalg.cho_solve((factor, True), columns)
    new_left = first[0] - dot_against(solved, cross_left)
    new_cross = -dot_high(solved, cross_right)
    new_right = second[2] - dot_leading(weights, cross_right)
    return jnp.stack([new_left, new_cross, new_right])


def shards(row_owner, face_left, face_cross, face_right):
    rows = face_left.shape[2]
    width = face_left.shape[3]
    mine = jnp.stack([face_left[0, 0], face_cross[0, 0], face_right[0, 0]])
    mine = jnp.take(mine, row_owner, axis=2)
    inverse_map = (
        jnp.zeros((width,), jnp.int32).at[row_owner].set(jnp.arange(width, dtype=jnp.int32))
    )
    start = lax.axis_index("leaf") * rows
    role_one = lax.axis_index("grp") % 2
    partner = partner_2(mine, "grp", 0)
    first, second = arrange(mine, partner, role_one)
    gathered = lax.all_gather(
        jnp.stack([first[2] + second[0], first[1], second[1]]), "leaf", axis=1, tiled=True
    )
    factor = jnp.linalg.cholesky(gathered[0])
    crossing = gathered[1:]
    mine = merge_rows(first, second, factor, crossing[0], crossing[1], start)
    role_two = lax.axis_index("mrg") % 2
    partner = partner_2(mine, "mrg", 0)
    first, second = arrange(mine, partner, role_two)
    gathered = lax.all_gather(
        jnp.stack([first[2] + second[0], first[1], second[1]]), "leaf", axis=1, tiled=True
    )
    factor = jnp.linalg.cholesky(gathered[0])
    crossing = gathered[1:]
    mine = merge_rows(first, second, factor, crossing[0], crossing[1], start)
    mine = jnp.take(mine, inverse_map, axis=2)
    return (mine[0][None, None], mine[1][None, None], mine[2][None, None])


def solution(mesh):
    in_specs = (
        P(),
        P("grp", "mrg", "leaf", None),
        P("grp", "mrg", "leaf", None),
        P("grp", "mrg", "leaf", None),
    )
    out_specs = (
        P("grp", "mrg", "leaf", None),
        P("grp", "mrg", "leaf", None),
        P("grp", "mrg", "leaf", None),
    )
    return jax.shard_map(shards, mesh=mesh, in_specs=in_specs, out_specs=out_specs, check_vma=False)
```

profile of v0, /device:TPU:4, one launch (start us, length us, event | category | flops | bytes accessed | tf_op | source)
XLA Modules:
  0.0 837.3 jit_solution(3703308753409520388)
XLA Ops:
  10.4 3.4 scatter_custom_fusion
  13.8 2.8 gather_fusion
  17.2 15.7 %collective-permute-start = (f32[3,48,768]{2,1,0:T(8,128)S(1)}, f32[3,48,768]{2,1,0:T(8,128)S(1)}, u32[]{:S(2)}, u32[]{:S(2)}) collective-permute-start(f32[3,48,768]{2,1,0:T(8,128)S(1)} %select_bitcast_fusion.1), channel_id=1, source_target_pairs={{0,4},{4,0},{8,12},{12,8},{16,20},{20,16},{24,28},{28,24},{1,5},{5... | collective-permute-start | bytes 1327112 | tf_op jit(solution)/shard_map/ppermute | solution.py:14
  33.0 14.7 %collective-permute-done = f32[3,48,768]{2,1,0:T(8,128)S(1)} collective-permute-done((f32[3,48,768]{2,1,0:T(8,128)S(1)}, f32[3,48,768]{2,1,0:T(8,128)S(1)}, u32[]{:S(2)}, u32[]{:S(2)}) %collective-permute-start) | collective-permute-done | bytes 442400 | tf_op jit(solution)/shard_map/ppermute | solution.py:14
  49.6 138.4 %all-gather.3.cloned.1.call-done = f32[3,768,768]{2,1,0:T(8,128)} async-done(((f32[3,48,768]{2,1,0:T(8,128)}), f32[3,768,768]{2,1,0:T(8,128)}) %all-gather.3.cloned.1.call-update) | async-done | bytes 7077904 | tf_op jit(solution)/shard_map/all_gather | solution.py:70
  188.0 4.1 fusion.325
  193.1 2.2 copy.46
  195.3 2.0 fusion.3
  198.7 11.7 %cholesky.453 = f32[128,128]{1,0:T(8,128)S(1)} custom-call(f32[128,128]{1,0:T(8,128)S(1)} %cholesky.669), custom_call_target="Cholesky" | custom-call | tf_op jit(solution)/shard_map/jit(cholesky)/cholesky | solution.py:73
  210.6 9.8 %custom-call.45 = f32[1,128,128]{1,2,0:T(8,128)S(1)} custom-call(f32[1,128,128]{2,1,0:T(8,128)S(1)} %get-tuple-element.115), custom_call_target="InvertDiagBlocksLowerTriangular" | custom-call | tf_op jit(solution)/shard_map/jit(cholesky)/cholesky | solution.py:73
  223.3 11.7 %cholesky.472 = f32[128,128]{1,0:T(8,128)S(1)} custom-call(f32[128,128]{1,0:T(8,128)S(1)} %cholesky.673), custom_call_target="Cholesky" | custom-call | tf_op jit(solution)/shard_map/jit(cholesky)/cholesky | solution.py:73
  235.0 10.0 %custom-call.46 = f32[1,128,128]{1,2,0:T(8,128)S(1)} custom-call(f32[1,128,128]{2,1,0:T(8,128)S(1)} %get-tuple-element.112), custom_call_target="InvertDiagBlocksLowerTriangular" | custom-call | tf_op jit(solution)/shard_map/jit(cholesky)/cholesky | solution.py:73
  247.0 11.7 %cholesky.493 = f32[128,128]{1,0:T(8,128)S(1)} custom-call(f32[128,128]{1,0:T(8,128)S(1)} %cholesky.678), custom_call_target="Cholesky" | custom-call | tf_op jit(solution)/shard_map/jit(cholesky)/cholesky | solution.py:73
  258.7 9.8 %custom-call.47 = f32[1,128,128]{1,2,0:T(8,128)S(1)} custom-call(f32[1,128,128]{2,1,0:T(8,128)S(1)} %get-tuple-element.109), custom_call_target="InvertDiagBlocksLowerTriangular" | custom-call | tf_op jit(solution)/shard_map/jit(cholesky)/cholesky | solution.py:73
  268.8 1.6 convolution_subtract_fusion.5
  270.4 12.2 %cholesky.512 = f32[128,128]{1,0:T(8,128)S(1)} custom-call(f32[128,128]{1,0:T(8,128)S(1)} %cholesky.683), custom_call_target="Cholesky" | custom-call | tf_op jit(solution)/shard_map/jit(cholesky)/cholesky | solution.py:73
  282.6 9.8 %custom-call.48 = f32[1,128,128]{1,2,0:T(8,128)S(1)} custom-call(f32[1,128,128]{2,1,0:T(8,128)S(1)} %get-tuple-element.106), custom_call_target="InvertDiagBlocksLowerTriangular" | custom-call | tf_op jit(solution)/shard_map/jit(cholesky)/cholesky | solution.py:73
  294.2 11.7 %cholesky.531 = f32[128,128]{1,0:T(8,128)S(1)} custom-call(f32[128,128]{1,0:T(8,128)S(1)} %cholesky.688), custom_call_target="Cholesky" | custom-call | tf_op jit(solution)/shard_map/jit(cholesky)/cholesky | solution.py:73
  305.9 9.8 %custom-call.49 = f32[1,128,128]{1,2,0:T(8,128)S(1)} custom-call(f32[1,128,128]{2,1,0:T(8,128)S(1)} %get-tuple-element.103), custom_call_target="InvertDiagBlocksLowerTriangular" | custom-call | tf_op jit(solution)/shard_map/jit(cholesky)/cholesky | solution.py:73
  317.3 11.9 %cholesky.548 = f32[128,128]{1,0:T(8,128)S(1)} custom-call(f32[128,128]{1,0:T(8,128)S(1)} %convolution_subtract_fusion.9), custom_call_target="Cholesky" | custom-call | tf_op jit(solution)/shard_map/jit(cholesky)/cholesky | solution.py:73
  337.2 3.4 select_select_fusion.1
  340.6 17.9 %while.8 = (s32[]{:T(128)}, f32[768,768]{1,0:T(8,128)}, s32[6,2]{0,1:T(2,128)S(1)}, f32[6,128,128]{2,1,0:T(8,128)S(1)}, s32[]{:T(128)}) while((s32[]{:T(128)}, f32[768,768]{1,0:T(8,128)}, s32[6,2]{0,1:T(2,128)S(1)}, f32[6,128,128]{2,1,0:T(8,128)S(1)}, s32[]{:T(128)}) %tuple.109), condition=%wide.while_cond, body=%wide.while_body.sunk | while | flops 2 | bytes 131189 | solution.py:50
  341.3 2.3 bitcast_dynamic-update-slice_fusion.4
  344.3 2.3 bitcast_dynamic-update-slice_fusion.4
  347.3 2.3 bitcast_dynamic-update-slice_fusion.4
  350.3 2.3 bitcast_dynamic-update-slice_fusion.4
  353.3 2.3 bitcast_dynamic-update-slice_fusion.4
  356.3 2.2 bitcast_dynamic-update-slice_fusion.4
  359.3 59.8 %custom-call.50 = f32[6,128,128]{1,2,0:T(8,128)S(1)} custom-call(f32[6,128,128]{2,1,0:T(8,128)} %copy-done.11), custom_call_target="InvertDiagBlocksLowerTriangular" | custom-call | tf_op jit(solution)/shard_map/jit(_cho_solve)/triangular_solve | solution.py:50
  425.7 1.6 convolution_subtract_fusion.36
  437.5 3.2 fusion.81
  440.7 2.4 fusion.79
  443.2 2.7 collective-permute-start.1
  445.9 7.4 collective-permute-done.1
  455.2 109.9 %all-gather.5.cloned.1.call-done = f32[3,768,768]{2,1,0:T(8,128)} async-done(((f32[3,48,768]{2,1,0:T(8,128)}), f32[3,768,768]{2,1,0:T(8,128)}) %all-gather.5.cloned.1.call-update) | async-done | bytes 7077904 | tf_op jit(solution)/shard_map/all_gather | solution.py:79
  565.2 4.1 fusion.324
  570.3 2.4 copy.47
  572.7 2.0 fusion.2
  576.2 11.7 %cholesky.563 = f32[128,128]{1,0:T(8,128)S(1)} custom-call(f32[128,128]{1,0:T(8,128)S(1)} %cholesky.692), custom_call_target="Cholesky" | custom-call | tf_op jit(solution)/shard_map/jit(cholesky)/cholesky | solution.py:82
  588.1 9.8 %custom-call.52 = f32[1,128,128]{1,2,0:T(8,128)S(1)} custom-call(f32[1,128,128]{2,1,0:T(8,128)S(1)} %get-tuple-element.99), custom_call_target="InvertDiagBlocksLowerTriangular" | custom-call | tf_op jit(solution)/shard_map/jit(cholesky)/cholesky | solution.py:82
  600.7 11.7 %cholesky.582 = f32[128,128]{1,0:T(8,128)S(1)} custom-call(f32[128,128]{1,0:T(8,128)S(1)} %cholesky.696), custom_call_target="Cholesky" | custom-call | tf_op jit(solution)/shard_map/jit(cholesky)/cholesky | solution.py:82
  612.4 10.0 %custom-call.53 = f32[1,128,128]{1,2,0:T(8,128)S(1)} custom-call(f32[1,128,128]{2,1,0:T(8,128)S(1)} %get-tuple-element.96), custom_call_target="InvertDiagBlocksLowerTriangular" | custom-call | tf_op jit(solution)/shard_map/jit(cholesky)/cholesky | solution.py:82
  624.3 11.7 %cholesky.603 = f32[128,128]{1,0:T(8,128)S(1)} custom-call(f32[128,128]{1,0:T(8,128)S(1)} %cholesky.701), custom_call_target="Cholesky" | custom-call | tf_op jit(solution)/shard_map/jit(cholesky)/cholesky | solution.py:82
  636.1 9.8 %custom-call.54 = f32[1,128,128]{1,2,0:T(8,128)S(1)} custom-call(f32[1,128,128]{2,1,0:T(8,128)S(1)} %get-tuple-element.93), custom_call_target="InvertDiagBlocksLowerTriangular" | custom-call | tf_op jit(solution)/shard_map/jit(cholesky)/cholesky | solution.py:82
  646.2 1.6 convolution_subtract_fusion.4
  647.8 12.1 %cholesky.622 = f32[128,128]{1,0:T(8,128)S(1)} custom-call(f32[128,128]{1,0:T(8,128)S(1)} %cholesky.706), custom_call_target="Cholesky" | custom-call | tf_op jit(solution)/shard_map/jit(cholesky)/cholesky | solution.py:82
  659.9 9.8 %custom-call.55 = f32[1,128,128]{1,2,0:T(8,128)S(1)} custom-call(f32[1,128,128]{2,1,0:T(8,128)S(1)} %get-tuple-element.90), custom_call_target="InvertDiagBlocksLowerTriangular" | custom-call | tf_op jit(solution)/shard_map/jit(cholesky)/cholesky | solution.py:82
  671.5 11.7 %cholesky.641 = f32[128,128]{1,0:T(8,128)S(1)} custom-call(f32[128,128]{1,0:T(8,128)S(1)} %cholesky.711), custom_call_target="Cholesky" | custom-call | tf_op jit(solution)/shard_map/jit(cholesky)/cholesky | solution.py:82
  683.3 9.8 %custom-call.56 = f32[1,128,128]{1,2,0:T(8,128)S(1)} custom-call(f32[1,128,128]{2,1,0:T(8,128)S(1)} %get-tuple-element.87), custom_call_target="InvertDiagBlocksLowerTriangular" | custom-call | tf_op jit(solution)/shard_map/jit(cholesky)/cholesky | solution.py:82
  694.6 11.7 %cholesky.658 = f32[128,128]{1,0:T(8,128)S(1)} custom-call(f32[128,128]{1,0:T(8,128)S(1)} %convolution_subtract_fusion.8), custom_call_target="Cholesky" | custom-call | tf_op jit(solution)/shard_map/jit(cholesky)/cholesky | solution.py:82
  714.4 3.4 select_select_fusion
  717.8 18.1 %while.9 = (s32[]{:T(128)}, f32[768,768]{1,0:T(8,128)}, s32[6,2]{0,1:T(2,128)S(1)}, f32[6,128,128]{2,1,0:T(8,128)S(1)}, s32[]{:T(128)}) while((s32[]{:T(128)}, f32[768,768]{1,0:T(8,128)}, s32[6,2]{0,1:T(2,128)S(1)}, f32[6,128,128]{2,1,0:T(8,128)S(1)}, s32[]{:T(128)}) %tuple.119), condition=%wide.while_cond.clone.1, body=%wide.while_body.clone.1.sunk | while | flops 2 | bytes 131189 | solution.py:50
  718.5 2.3 bitcast_dynamic-update-slice_fusion.5
  721.5 2.3 bitcast_dynamic-update-slice_fusion.5
  724.5 2.3 bitcast_dynamic-update-slice_fusion.5
  727.5 2.3 bitcast_dynamic-update-slice_fusion.5
  730.6 2.3 bitcast_dynamic-update-slice_fusion.5
  733.6 2.3 bitcast_dynamic-update-slice_fusion.5
  736.6 59.9 %custom-call.57 = f32[6,128,128]{1,2,0:T(8,128)S(1)} custom-call(f32[6,128,128]{2,1,0:T(8,128)} %copy-done.10), custom_call_target="InvertDiagBlocksLowerTriangular" | custom-call | tf_op jit(solution)/shard_map/jit(_cho_solve)/triangular_solve | solution.py:50
  803.3 1.6 convolution_subtract_fusion.30
  815.0 3.2 fusion.77
  818.2 2.4 fusion.75
  821.4 2.8 gather_fusion.1
  824.2 2.8 select_bitcast_fusion
  (271 shorter events, 84.2 us)
Async XLA Ops:
  7.2 180.8 %all-gather.3.cloned.1.call-start = ((), (), s32[]{:S(2)}) async-start(), calls=%async_computation | async-start | bytes 7520256 | tf_op jit(solution)/shard_map/all_gather | solution.py:70
  17.2 30.4 %collective-permute-start = (f32[3,48,768]{2,1,0:T(8,128)S(1)}, f32[3,48,768]{2,1,0:T(8,128)S(1)}, u32[]{:S(2)}, u32[]{:S(2)}) collective-permute-start(f32[3,48,768]{2,1,0:T(8,128)S(1)} %select_bitcast_fusion.1), channel_id=1, source_target_pairs={{0,4},{4,0},{8,12},{12,8},{16,20},{20,16},{24,28},{28,24},{1,5},{5... | collective-permute-start | bytes 1327112 | tf_op jit(solution)/shard_map/ppermute | solution.py:14
  47.8 0.8 copy-start.6
  47.8 0.9 copy-start.7
  49.5 515.6 %all-gather.5.cloned.1.call-start = ((), (), s32[]{:S(2)}) async-start(), calls=%async_computation.1 | async-start | bytes 7520256 | tf_op jit(solution)/shard_map/all_gather | solution.py:79
  197.3 1.5 copy-start.4
  329.2 8.0 copy-start
  337.2 98.8 %slice-start = ((s8[7077888]{0:T(1024)(128)(4,1)}), s8[2883584]{0:T(1024)(128)(4,1)S(1)}, s32[]{:S(2)}) async-start(s8[7077888]{0:T(1024)(128)(4,1)} %bitcast.376), calls=%async_computation.2 | async-start | bytes 5767168
  358.5 0.7 copy-start.11
  419.0 8.8 %copy-start.3 = (f32[768,768]{1,0:T(8,128)S(1)}, f32[768,768]{1,0:T(8,128)}, u32[]{:S(2)}) copy-start(f32[768,768]{1,0:T(8,128)} %get-tuple-element.263) | copy-start | bytes 7077892
  425.7 10.2 %slice-start.1 = ((s8[7077888]{0:T(1024)(128)(4,1)}), s8[4194304]{0:T(1024)(128)(4,1)S(1)}, s32[]{:S(2)}) async-start(s8[7077888]{0:T(1024)(128)(4,1)} %bitcast.376), calls=%async_computation.3 | async-start | bytes 8388608
  443.2 10.2 %collective-permute-start.1 = (f32[3,48,768]{2,1,0:T(8,128)S(1)}, f32[3,48,768]{2,1,0:T(8,128)S(1)}, u32[]{:S(2)}, u32[]{:S(2)}) collective-permute-start(f32[3,48,768]{2,1,0:T(8,128)S(1)} %pad_maximum_fusion.2), channel_id=1, source_target_pairs={{0,1},{1,0},{2,3},{3,2},{4,5},{5,4},{6,7},{7,6},{8,9},{9,8},{10,11... | collective-permute-start | bytes 1327112 | tf_op jit(solution)/shard_map/ppermute | solution.py:14
  453.4 0.8 copy-start.8
  453.4 0.9 copy-start.9
  574.7 1.5 copy-start.5
  706.4 8.0 copy-start.1
  714.3 99.2 %slice-start.2 = ((s8[7077888]{0:T(1024)(128)(4,1)}), s8[2883584]{0:T(1024)(128)(4,1)S(1)}, s32[]{:S(2)}) async-start(s8[7077888]{0:T(1024)(128)(4,1)} %bitcast.378), calls=%async_computation.4 | async-start | bytes 5767168
  735.9 0.7 copy-start.10
  796.6 8.7 %copy-start.2 = (f32[768,768]{1,0:T(8,128)S(1)}, f32[768,768]{1,0:T(8,128)}, u32[]{:S(2)}) copy-start(f32[768,768]{1,0:T(8,128)} %get-tuple-element.262) | copy-start | bytes 7077892
  803.3 10.2 %slice-start.3 = ((s8[7077888]{0:T(1024)(128)(4,1)}), s8[4194304]{0:T(1024)(128)(4,1)S(1)}, s32[]{:S(2)}) async-start(s8[7077888]{0:T(1024)(128)(4,1)} %bitcast.378), calls=%async_computation.5 | async-start | bytes 8388608
Sparse Core Ops, SparseCore 0:
  49.6 138.2 all-gather.2
  455.3 109.7 all-gather.4
where the time goes:
time: 842 us; the launch traced here: 837 us
  other arithmetic  386 us (46%)
  waiting for transfers between devices  270 us (32%)
  local copies, waits for them, and re-layouts  71.6 us (9%)
  matrix products  66.5 us (8%)
  between operations  23.6 us (3%)
  starting transfers between devices  18.6 us (2%)
    another operation x46, other arithmetic, shards(): factor = jnp.linalg.cholesky(gathered[0])  249 us
    all_gather x2, waiting for transfers between devices, shards(): lax.all_gather(jnp.stack([first[2] + second[0], first[1], second[1]]), 'l...  248 us
    another operation x5, other arithmetic, merge_rows(): solved = jax.scipy.linalg.cho_solve((factor, True), first[1].T).T  126 us
    another operation x43, local copies, waits for them, and re-layouts, merge_rows(): solved = jax.scipy.linalg.cho_solve((factor, True), first[1].T).T  35.8 us
    ppermute x2, waiting for transfers between devices, partner_2(): return lax.ppermute(block, axis, route)  22.1 us
    another operation x44, matrix products, merge_rows(): weights = jax.scipy.linalg.cho_solve((factor, True), columns)  22 us
    another operation x20, matrix products, shards(): factor = jnp.linalg.cholesky(gathered[0])  19.6 us
    ppermute x2, starting transfers between devices, partner_2(): return lax.ppermute(block, axis, route)  18.5 us
  transfers between devices with their start and end apart: 4, of which 4 were waited for; matrix products, arithmetic and copies ran while one was open for 0% of the time, Pallas kernels for 0%

commit v1 on v0

--- a/solution.py
+++ b/solution.py
@@ -67,8 +67,16 @@
     role_one = lax.axis_index("grp") % 2
     partner = partner_2(mine, "grp", 0)
     first, second = arrange(mine, partner, role_one)
-    gathered = lax.all_gather(
-        jnp.stack([first[2] + second[0], first[1], second[1]]), "leaf", axis=1, tiled=True
+    gathered = jnp.concatenate(
+        lax.all_to_all(
+            jnp.stack(
+                [jnp.stack([first[2] + second[0], first[1], second[1]])] * lax.axis_size("leaf")
+            ),
+            "leaf",
+            0,
+            0,
+        ),
+        axis=1,
     )
     factor = jnp.linalg.cholesky(gathered[0])
     crossing = gathered[1:]

time: 842 us -> 1060 us (1.26)
  waiting for transfers between devices: 270 us -> 445 us
  starting transfers between devices: 18.6 us -> 50.1 us
    all_to_all x0 -> x1, waiting for transfers between devices: none -> 254 us  [shards(): lax.all_to_all(jnp.stack([jnp.stack([first[2] + second[0], first[1], seco...]
    all_gather x2 -> x1, waiting for transfers between devices: 248 us -> 165 us  [shards(): lax.all_gather(jnp.stack([first[2] + second[0], first[1], second[1]]), 'l...]
    all_to_all x0 -> x1, starting transfers between devices: none -> 31.2 us  [shards(): lax.all_to_all(jnp.stack([jnp.stack([first[2] + second[0], first[1], seco...]
where the time goes in v1:
time: 1060 us
  waiting for transfers between devices  445 us (42%)
  other arithmetic  391 us (37%)
  local copies, waits for them, and re-layouts  77.1 us (7%)
  matrix products  72.6 us (7%)
  starting transfers between devices  50.1 us (5%)
  between operations  23.2 us (2%)
    all_to_all x1, waiting for transfers between devices, shards(): lax.all_to_all(jnp.stack([jnp.stack([first[2] + second[0], first[1], seco...  254 us
    another operation x46, other arithmetic, shards(): factor = jnp.linalg.cholesky(gathered[0])  251 us
    all_gather x1, waiting for transfers between devices, shards(): lax.all_gather(jnp.stack([first[2] + second[0], first[1], second[1]]), 'l...  165 us
    another operation x5, other arithmetic, merge_rows(): solved = jax.scipy.linalg.cho_solve((factor, True), first[1].T).T  127 us
    another operation x43, local copies, waits for them, and re-layouts, merge_rows(): solved = jax.scipy.linalg.cho_solve((factor, True), first[1].T).T  34.1 us
    all_to_all x1, starting transfers between devices, shards(): lax.all_to_all(jnp.stack([jnp.stack([first[2] + second[0], first[1], seco...  31.2 us
    ppermute x2, waiting for transfers between devices, partner_2(): return lax.ppermute(block, axis, route)  26.5 us
    another operation x44, matrix products, merge_rows(): weights = jax.scipy.linalg.cho_solve((factor, True), columns)  24.4 us
  transfers between devices with their start and end apart: 4, of which 4 were waited for; matrix products, arithmetic and copies ran while one was open for 0% of the time, Pallas kernels for 0%

profile of v1, /device:TPU:4, one launch (start us, length us, event | category | flops | bytes accessed | tf_op | source)
XLA Modules:
  0.0 1059.0 jit_solution(5296946560435429019)
XLA Ops:
  10.4 3.4 scatter_custom_fusion
  14.3 2.8 gather_fusion
  17.8 15.7 %collective-permute-start = (f32[3,48,768]{2,1,0:T(8,128)S(1)}, f32[3,48,768]{2,1,0:T(8,128)S(1)}, u32[]{:S(2)}, u32[]{:S(2)}) collective-permute-start(f32[3,48,768]{2,1,0:T(8,128)S(1)} %select_bitcast_fusion.1), channel_id=1, source_target_pairs={{0,4},{4,0},{8,12},{12,8},{16,20},{20,16},{24,28},{28,24},{1,5},{5... | collective-permute-start | bytes 1327112 | tf_op jit(solution)/shard_map/ppermute | solution.py:14
  33.5 14.7 %collective-permute-done = f32[3,48,768]{2,1,0:T(8,128)S(1)} collective-permute-done((f32[3,48,768]{2,1,0:T(8,128)S(1)}, f32[3,48,768]{2,1,0:T(8,128)S(1)}, u32[]{:S(2)}, u32[]{:S(2)}) %collective-permute-start) | collective-permute-done | bytes 442400 | tf_op jit(solution)/shard_map/ppermute | solution.py:14
  49.1 3.8 stack.26
  52.9 31.2 %all-to-all-start = ((f32[16,3,48,768]{3,2,1,0:T(8,128)}), f32[16,3,48,768]{3,2,1,0:T(8,128)}, u32[]{:S(2)}, u32[]{:S(2)}) async-start(f32[16,3,48,768]{3,2,1,0:T(8,128)} %stack.26), calls=%async_computation | async-start | bytes 14155776 | tf_op jit(solution)/shard_map/all_to_all | solution.py:71
  84.8 253.6 %all-to-all-done = f32[16,3,48,768]{3,2,1,0:T(8,128)} async-done(((f32[16,3,48,768]{3,2,1,0:T(8,128)}), f32[16,3,48,768]{3,2,1,0:T(8,128)}, u32[]{:S(2)}, u32[]{:S(2)}) %all-to-all-start) | async-done | bytes 7077920 | tf_op jit(solution)/shard_map/all_to_all | solution.py:71
  338.4 3.5 copy.57
  341.8 2.6 fusion.312
  344.4 3.2 copy.38
  347.6 2.7 fusion.6
  351.7 11.7 %cholesky.453 = f32[128,128]{1,0:T(8,128)S(1)} custom-call(f32[128,128]{1,0:T(8,128)S(1)} %cholesky.669), custom_call_target="Cholesky" | custom-call | tf_op jit(solution)/shard_map/jit(cholesky)/cholesky | solution.py:81
  365.1 9.8 custom-call.45
  374.9 2.2 constant_dynamic-update-slice_fusion.69
  378.5 11.7 %cholesky.472 = f32[128,128]{1,0:T(8,128)S(1)} custom-call(f32[128,128]{1,0:T(8,128)S(1)} %cholesky.673), custom_call_target="Cholesky" | custom-call | tf_op jit(solution)/shard_map/jit(cholesky)/cholesky | solution.py:81
  390.8 10.2 custom-call.46
  403.9 11.7 %cholesky.493 = f32[128,128]{1,0:T(8,128)S(1)} custom-call(f32[128,128]{1,0:T(8,128)S(1)} %cholesky.678), custom_call_target="Cholesky" | custom-call | tf_op jit(solution)/shard_map/jit(cholesky)/cholesky | solution.py:81
  416.3 9.8 custom-call.47
  429.0 11.9 %cholesky.512 = f32[128,128]{1,0:T(8,128)S(1)} custom-call(f32[128,128]{1,0:T(8,128)S(1)} %cholesky.683), custom_call_target="Cholesky" | custom-call | tf_op jit(solution)/shard_map/jit(cholesky)/cholesky | solution.py:81
  441.5 9.8 custom-call.48
  454.0 11.7 %cholesky.531 = f32[128,128]{1,0:T(8,128)S(1)} custom-call(f32[128,128]{1,0:T(8,128)S(1)} %cholesky.688), custom_call_target="Cholesky" | custom-call | tf_op jit(solution)/shard_map/jit(cholesky)/cholesky | solution.py:81
  466.3 9.8 custom-call.49
  478.6 11.7 %cholesky.548 = f32[128,128]{1,0:T(8,128)S(1)} custom-call(f32[128,128]{1,0:T(8,128)S(1)} %convolution_subtract_fusion.9), custom_call_target="Cholesky" | custom-call | tf_op jit(solution)/shard_map/jit(cholesky)/cholesky | solution.py:81
  498.6 3.3 select_select_fusion.1
  501.9 16.9 %while.8 = (s32[]{:T(128)}, f32[768,768]{1,0:T(8,128)}, s32[6,2]{0,1:T(2,128)S(1)}, f32[6,128,128]{2,1,0:T(8,128)S(1)}, s32[]{:T(128)}) while((s32[]{:T(128)}, f32[768,768]{1,0:T(8,128)}, s32[6,2]{0,1:T(2,128)S(1)}, f32[6,128,128]{2,1,0:T(8,128)S(1)}, s32[]{:T(128)}) %tuple.114), condition=%wide.while_cond, body=%wide.while_body.sunk | while | flops 2 | bytes 131189 | solution.py:50
  502.5 2.2 bitcast_dynamic-update-slice_fusion.4
  505.3 2.2 bitcast_dynamic-update-slice_fusion.4
  508.1 2.2 bitcast_dynamic-update-slice_fusion.4
  511.0 2.2 bitcast_dynamic-update-slice_fusion.4
  513.8 2.2 bitcast_dynamic-update-slice_fusion.4
  516.6 2.1 bitcast_dynamic-update-slice_fusion.4
  519.5 60.2 %custom-call.50 = f32[6,128,128]{1,2,0:T(8,128)S(1)} custom-call(f32[6,128,128]{2,1,0:T(8,128)} %copy-done.11), custom_call_target="InvertDiagBlocksLowerTriangular" | custom-call | tf_op jit(solution)/shard_map/jit(_cho_solve)/triangular_solve | solution.py:50
  594.5 2.4 fusion.69
  604.0 2.3 fusion.71
  606.4 3.1 collective-permute-start.1
  609.5 11.8 %collective-permute-done.1 = f32[3,48,768]{2,1,0:T(8,128)S(1)} collective-permute-done((f32[3,48,768]{2,1,0:T(8,128)S(1)}, f32[3,48,768]{2,1,0:T(8,128)S(1)}, u32[]{:S(2)}, u32[]{:S(2)}) %collective-permute-start.1) | collective-permute-done | bytes 442400 | tf_op jit(solution)/shard_map/ppermute | solution.py:14
  623.2 164.9 %all-gather.2.cloned.1.call-done = f32[3,768,768]{2,1,0:T(8,128)} async-done(((f32[3,48,768]{2,1,0:T(8,128)}), f32[3,768,768]{2,1,0:T(8,128)}) %all-gather.2.cloned.1.call-update) | async-done | bytes 7077904 | tf_op jit(solution)/shard_map/all_gather | solution.py:87
  788.1 4.1 fusion.311
  793.2 2.2 copy.54
  795.5 2.0 fusion.1
  798.9 11.7 %cholesky.563 = f32[128,128]{1,0:T(8,128)S(1)} custom-call(f32[128,128]{1,0:T(8,128)S(1)} %cholesky.692), custom_call_target="Cholesky" | custom-call | tf_op jit(solution)/shard_map/jit(cholesky)/cholesky | solution.py:90
  810.8 9.8 custom-call.52
  823.4 11.7 %cholesky.582 = f32[128,128]{1,0:T(8,128)S(1)} custom-call(f32[128,128]{1,0:T(8,128)S(1)} %cholesky.696), custom_call_target="Cholesky" | custom-call | tf_op jit(solution)/shard_map/jit(cholesky)/cholesky | solution.py:90
  835.2 10.2 custom-call.53
  847.3 11.7 %cholesky.603 = f32[128,128]{1,0:T(8,128)S(1)} custom-call(f32[128,128]{1,0:T(8,128)S(1)} %cholesky.701), custom_call_target="Cholesky" | custom-call | tf_op jit(solution)/shard_map/jit(cholesky)/cholesky | solution.py:90
  859.0 9.8 custom-call.54
  870.7 11.9 %cholesky.622 = f32[128,128]{1,0:T(8,128)S(1)} custom-call(f32[128,128]{1,0:T(8,128)S(1)} %cholesky.706), custom_call_target="Cholesky" | custom-call | tf_op jit(solution)/shard_map/jit(cholesky)/cholesky | solution.py:90
  882.7 9.8 custom-call.55
  894.2 11.7 %cholesky.641 = f32[128,128]{1,0:T(8,128)S(1)} custom-call(f32[128,128]{1,0:T(8,128)S(1)} %cholesky.711), custom_call_target="Cholesky" | custom-call | tf_op jit(solution)/shard_map/jit(cholesky)/cholesky | solution.py:90
  906.0 9.8 custom-call.56
  917.3 11.7 %cholesky.658 = f32[128,128]{1,0:T(8,128)S(1)} custom-call(f32[128,128]{1,0:T(8,128)S(1)} %convolution_subtract_fusion.8), custom_call_target="Cholesky" | custom-call | tf_op jit(solution)/shard_map/jit(cholesky)/cholesky | solution.py:90
  936.6 3.5 select_select_fusion
  940.1 17.4 %while.9 = (s32[]{:T(128)}, f32[768,768]{1,0:T(8,128)}, s32[6,2]{0,1:T(2,128)S(1)}, f32[6,128,128]{2,1,0:T(8,128)S(1)}, s32[]{:T(128)}) while((s32[]{:T(128)}, f32[768,768]{1,0:T(8,128)}, s32[6,2]{0,1:T(2,128)S(1)}, f32[6,128,128]{2,1,0:T(8,128)S(1)}, s32[]{:T(128)}) %tuple.122), condition=%wide.while_cond.clone.1, body=%wide.while_body.clone.1.sunk | while | flops 2 | bytes 131189 | solution.py:50
  940.7 2.3 bitcast_dynamic-update-slice_fusion.5
  943.7 2.3 bitcast_dynamic-update-slice_fusion.5
  946.6 2.3 bitcast_dynamic-update-slice_fusion.5
  949.5 2.3 bitcast_dynamic-update-slice_fusion.5
  952.4 2.3 bitcast_dynamic-update-slice_fusion.5
  955.3 2.2 bitcast_dynamic-update-slice_fusion.5
  958.3 60.0 %custom-call.57 = f32[6,128,128]{1,2,0:T(8,128)S(1)} custom-call(f32[6,128,128]{2,1,0:T(8,128)} %copy-done.10), custom_call_target="InvertDiagBlocksLowerTriangular" | custom-call | tf_op jit(solution)/shard_map/jit(_cho_solve)/triangular_solve | solution.py:50
  1036.7 3.2 fusion.67
  1039.9 2.4 fusion.65
  1043.1 2.8 gather_fusion.1
  1046.0 2.8 select_bitcast_fusion
  (275 shorter events, 98.8 us)
Async XLA Ops:
  17.8 30.4 %collective-permute-start = (f32[3,48,768]{2,1,0:T(8,128)S(1)}, f32[3,48,768]{2,1,0:T(8,128)S(1)}, u32[]{:S(2)}, u32[]{:S(2)}) collective-permute-start(f32[3,48,768]{2,1,0:T(8,128)S(1)} %select_bitcast_fusion.1), channel_id=1, source_target_pairs={{0,4},{4,0},{8,12},{12,8},{16,20},{20,16},{24,28},{28,24},{1,5},{5... | collective-permute-start | bytes 1327112 | tf_op jit(solution)/shard_map/ppermute | solution.py:14
  48.3 4.6 copy-start.6
  52.9 285.5 %all-to-all-start = ((f32[16,3,48,768]{3,2,1,0:T(8,128)}), f32[16,3,48,768]{3,2,1,0:T(8,128)}, u32[]{:S(2)}, u32[]{:S(2)}) async-start(f32[16,3,48,768]{3,2,1,0:T(8,128)} %stack.26), calls=%async_computation | async-start | bytes 14155776 | tf_op jit(solution)/shard_map/all_to_all | solution.py:71
  84.1 704.0 %all-gather.2.cloned.1.call-start = ((), (), s32[]{:S(2)}) async-start(), calls=%async_computation.1 | async-start | bytes 7520256 | tf_op jit(solution)/shard_map/all_gather | solution.py:87
  350.3 1.4 copy-start.4
  498.6 3.3 copy-start.13
  518.8 0.8 copy-start.11
  581.8 10.1 copy-start.1
  592.8 4.1 copy-start.9
  600.8 3.2 copy-start.3
  606.4 14.9 %collective-permute-start.1 = (f32[3,48,768]{2,1,0:T(8,128)S(1)}, f32[3,48,768]{2,1,0:T(8,128)S(1)}, u32[]{:S(2)}, u32[]{:S(2)}) collective-permute-start(f32[3,48,768]{2,1,0:T(8,128)S(1)} %pad_maximum_fusion.2), channel_id=1, source_target_pairs={{0,1},{1,0},{2,3},{3,2},{4,5},{5,4},{6,7},{7,6},{8,9},{9,8},{10,11... | collective-permute-start | bytes 1327112 | tf_op jit(solution)/shard_map/ppermute | solution.py:14
  621.4 0.8 copy-start.7
  621.4 0.9 copy-start.8
  797.4 1.5 copy-start.5
  929.1 7.5 copy-start
  936.6 98.6 %slice-start = ((s8[7077888]{0:T(1024)(128)(4,1)}), s8[2883584]{0:T(1024)(128)(4,1)S(1)}, s32[]{:S(2)}) async-start(s8[7077888]{0:T(1024)(128)(4,1)} %bitcast.366), calls=%async_computation.2 | async-start | bytes 5767168
  957.5 0.7 copy-start.10
  1018.2 8.7 copy-start.2
  1025.0 10.2 slice-start.1
  1039.9 3.2 copy-start.12
Sparse Core Ops, SparseCore 0:
  623.3 164.7 all-gather.1
